TPU v7x, 32 devices: a whole 2x2x4 slice. The times are simulated.
32 devices in a mesh: seq: 4 (over z), wt: 8 (over y, x, core).
Axes of the slice: x: 2, y: 2, z: 4, core: 2. Of those that a mesh axis runs over, the one named last changes fastest.
Arguments:
- tokens: bfloat16 [8, 512, 2048], P('wt', 'seq'), may hold values from -6 to 6
- cotangent: bfloat16 [8, 512, 2048], P('wt', 'seq'), may hold values from -6 to 6
- segment_ids: int32 [8, 512], P('wt'), may hold values from 0 to 1, never falling along the last dimension, each value on 1 to 320 neighbouring positions
- expert_routes: int32 [8, 512, 8], P('wt', 'seq'), may hold values from 0 to 15, all different within a row; in each aligned block of 128 rows (0 to 127, 128 to 255, ..., all dimensions but the last counted through in order) at most 128 rows name the same one
- w_qkv: bfloat16 [2048, 6144], P('wt'), may hold values from -0.125 to 0.125
- w_out: bfloat16 [2048, 2048], P('wt'), may hold values from -2 to 2
- w_router: bfloat16 [2048, 16], P('wt'), may hold values from -0.0625 to 0.0625
- w_gate_up: bfloat16 [16, 2048, 2048], P('seq', 'wt'), may hold values from -0.125 to 0.125
- w_down: bfloat16 [16, 1024, 2048], P('seq', 'wt'), may hold values from -0.75 to 0.75
- attn_gain: bfloat16 [2048], P('wt'), may hold values from 0.5 to 1.5
- ffn_gain: bfloat16 [2048], P('wt'), may hold values from 0.5 to 1.5
- q_gain: bfloat16 [128], P('wt'), may hold values from 0.5 to 1.5
- k_gain: bfloat16 [128], P('wt'), may hold values from 0.5 to 1.5
Outputs:
- output: bfloat16 [8, 512, 2048], P('wt', 'seq')
- tokens_grad: float32 [8, 512, 2048], P('wt', 'seq')
- w_qkv_grad: float32 [2048, 6144], P('wt')
- w_out_grad: float32 [2048, 2048], P('wt')
- w_router_grad: float32 [2048, 16], P('wt')
- w_gate_up_grad: float32 [16, 2048, 2048], P('seq', 'wt')
- w_down_grad: float32 [16, 1024, 2048], P('seq', 'wt')
- attn_gain_grad: float32 [2048], P('wt')
- ffn_gain_grad: float32 [2048], P('wt')
- q_gain_grad: float32 [128], P('wt')
- k_gain_grad: float32 [128], P('wt')
Inputs may be any that keep to these rules, and one draw needn't show every extreme that they name: `segment_ids`: along a sequence the segment numbers never fall; each of the 2 documents spans 1 to 320 positions. `expert_routes`: A token names 8 different experts; among the 128 tokens of one device no expert is named more than 128 times, a bound that some block reaches.
All inputs are finite; a program needn't handle non-finite values.
Results may differ from a plain program's by a relative error of at most 0.028.
Values may be sent and summed in bfloat16 or wider, within the bound.
A program may use at most 512 MiB of HBM per device.

v0:
```python
import jax
import jax.numpy as jnp
from jax import lax
from jax.sharding import PartitionSpec as P

H = 16
HD = 128
FF = 1024


EPS = 1e-06
THETA = 50000.0
NEG = -1e30


def normalize(values):
    factor = lax.rsqrt(jnp.mean(values * values, axis=-1, keepdims=True) + EPS)
    return (values * factor, factor)


def norm_back(grad_normed, normed_values, factor):
    return factor * (
        grad_normed - normed_values * jnp.mean(grad_normed * normed_values, axis=-1, keepdims=True)
    )


def rotate(values, positions, sign):
    half = values.shape[-1] // 2
    freq = THETA ** (-jnp.arange(half, dtype=jnp.float32) * 2.0 / values.shape[-1])
    angle = positions.astype(jnp.float32)[:, None] * freq[None, :]
    cosine = jnp.cos(angle)[:, None, :]
    sine = sign * jnp.sin(angle)[:, None, :]
    first = values[..., :half]
    second = values[..., half:]
    return jnp.concatenate(
        [first * cosine - second * sine, second * cosine + first * sine], axis=-1
    )


def scores(query_block, key_one, segment_block, segments):
    raw = jnp.dot(query_block, key_one.T, preferred_element_type=jnp.float32) * HD ** (-0.5)
    return jnp.where(segment_block[:, None] == segments[None, :], raw, NEG)


def body(
    tokens,
    cotangent,
    segment_ids,
    expert_routes,
    w_qkv,
    w_out,
    w_router,
    w_gate_up,
    w_down,
    attn_gain,
    ffn_gain,
    q_gain,
    k_gain,
):
    seq_total = lax.axis_size("seq")
    gathered = (
        lax.all_gather(w_qkv, "wt", axis=0, tiled=True),
        lax.all_gather(w_out, "wt", axis=0, tiled=True),
        lax.all_gather(w_router, "wt", axis=0, tiled=True),
        lax.all_gather(attn_gain, "wt", axis=0, tiled=True),
        lax.all_gather(ffn_gain, "wt", axis=0, tiled=True),
        lax.all_gather(q_gain, "wt", axis=0, tiled=True),
        lax.all_gather(k_gain, "wt", axis=0, tiled=True),
    )
    qkv_full = gathered[0]
    out_full = gathered[1]
    router_full = gathered[2]
    gain_attn = gathered[3].astype(jnp.float32)
    gain_ffn = gathered[4].astype(jnp.float32)
    gain_query = gathered[5].astype(jnp.float32)
    gain_key = gathered[6].astype(jnp.float32)
    token_rows = tokens.shape[1]
    model_width = tokens.shape[2]
    expert_total = router_full.shape[1]
    local_experts = w_gate_up.shape[0]
    top_count = expert_routes.shape[2]
    capacity = 2 * token_rows * top_count // expert_total
    positions = lax.axis_index("seq") * token_rows + jnp.arange(token_rows, dtype=jnp.int32)
    segments = segment_ids[0]
    length = segments.shape[0]
    width = min(512, length)
    offsets = jnp.arange(length // width, dtype=jnp.int32) * width
    inputs = tokens[0].astype(jnp.float32)
    normed_a, factor_a = normalize(inputs)
    hidden = (normed_a * gain_attn).astype(jnp.bfloat16)
    projected = jnp.dot(hidden, qkv_full, preferred_element_type=jnp.float32).reshape(
        token_rows, 3, H, HD
    )
    normed_q, factor_q = normalize(projected[:, 0])
    normed_k, factor_k = normalize(projected[:, 1])
    queries = rotate(normed_q * gain_query, positions, 1.0)
    keys_all = rotate(normed_k * gain_key, positions, 1.0)
    stacked = jnp.stack([queries, keys_all, projected[:, 2]]).astype(jnp.bfloat16)
    by_head = lax.all_to_all(stacked, "seq", split_axis=2, concat_axis=1, tiled=True)
    query_heads = jnp.swapaxes(by_head[0], 0, 1)
    key_heads = jnp.swapaxes(by_head[1], 0, 1)
    value_heads = jnp.swapaxes(by_head[2], 0, 1)

    def forward_head(operands):
        query_one, key_one, value_one = operands

        def forward_block(offset):
            query_block = lax.dynamic_slice_in_dim(query_one, offset, width, 0)
            segment_block = lax.dynamic_slice_in_dim(segments, offset, width, 0)
            logits = scores(query_block, key_one, segment_block, segments)
            highest = jnp.max(logits, axis=-1, keepdims=True)
            powers = jnp.exp(logits - highest)
            totals = jnp.sum(powers, axis=-1, keepdims=True)
            weights = (powers / totals).astype(jnp.bfloat16)
            mixed = jnp.dot(weights, value_one, preferred_element_type=jnp.float32).astype(
                jnp.bfloat16
            )
            return (mixed, (highest + jnp.log(totals))[:, 0])

        mixed_all, log_all = lax.map(forward_block, offsets)
        return (mixed_all.reshape(length, HD), log_all.reshape(length))

    attended, log_totals = lax.map(forward_head, (query_heads, key_heads, value_heads))
    merged = lax.all_to_all(
        jnp.swapaxes(attended, 0, 1), "seq", split_axis=0, concat_axis=1, tiled=True
    ).reshape(token_rows, H * HD)
    residual = inputs + jnp.dot(merged, out_full, preferred_element_type=jnp.float32)
    normed_f, factor_f = normalize(residual)
    hidden_ffn = (normed_f * gain_ffn).astype(jnp.bfloat16)
    router_logits = jnp.dot(hidden_ffn, router_full, preferred_element_type=jnp.float32)
    chances = jax.nn.softmax(router_logits, axis=-1)
    routes = expert_routes[0]
    picked = jnp.take_along_axis(chances, routes, axis=1)
    picked_total = jnp.sum(picked, axis=1, keepdims=True)
    gate_values = picked / picked_total
    flat_routes = routes.reshape(-1)
    assign_count = flat_routes.shape[0]
    onehot_table = (
        flat_routes[:, None] == jnp.arange(expert_total, dtype=jnp.int32)[None, :]
    ).astype(jnp.int32)
    ranks = jnp.sum((jnp.cumsum(onehot_table, axis=0) - 1) * onehot_table, axis=1)
    slots = flat_routes * capacity + ranks
    owners = (
        jnp.zeros((expert_total * capacity,), jnp.int32)
        .at[slots]
        .set(jnp.arange(assign_count, dtype=jnp.int32))
    )
    filled = jnp.zeros((expert_total * capacity,), jnp.int32).at[slots].set(1) > 0
    sources = owners // top_count
    sent_rows = jnp.where(filled[:, None], hidden_ffn[sources], jnp.zeros((), jnp.bfloat16))
    expert_full = (
        lax.all_gather(w_gate_up, "wt", axis=1, tiled=True),
        lax.all_gather(w_down, "wt", axis=1, tiled=True),
    )
    gate_up_full = expert_full[0]
    down_full = expert_full[1]
    arrived = lax.all_to_all(
        sent_rows.reshape(seq_total, local_experts, capacity, model_width),
        "seq",
        split_axis=0,
        concat_axis=0,
        tiled=True,
    )
    gate_up = jnp.einsum(
        "secd,edf->secf", arrived, gate_up_full, preferred_element_type=jnp.float32
    )
    gate_part = gate_up[..., :FF]
    up_part = gate_up[..., FF:]
    sigmoid_gate = jax.nn.sigmoid(gate_part)
    activated = (gate_part * sigmoid_gate * up_part).astype(jnp.bfloat16)
    expert_out = jnp.einsum(
        "secf,efd->secd", activated, down_full, preferred_element_type=jnp.float32
    ).astype(jnp.bfloat16)
    returned = lax.all_to_all(expert_out, "seq", split_axis=0, concat_axis=0, tiled=True).reshape(
        expert_total * capacity, model_width
    )
    picked_rows = returned[slots].reshape(token_rows, top_count, model_width).astype(jnp.float32)
    output = residual + jnp.sum(gate_values[:, :, None] * picked_rows, axis=1)
    grad_out = cotangent[0].astype(jnp.float32)
    grad_gates = jnp.sum(grad_out[:, None, :] * picked_rows, axis=-1)
    flat_gates = gate_values.reshape(-1)
    slot_grads = jnp.where(
        filled[:, None], flat_gates[owners][:, None] * grad_out[sources], 0.0
    ).astype(jnp.bfloat16)
    grad_arrived = lax.all_to_all(
        slot_grads.reshape(seq_total, local_experts, capacity, model_width),
        "seq",
        split_axis=0,
        concat_axis=0,
        tiled=True,
    )
    gate_up_grads = []
    down_grads = []
    row_grads = []
    for expert_index in range(local_experts):
        grad_here = grad_arrived[:, expert_index]
        gate_here = gate_part[:, expert_index]
        sigmoid_here = sigmoid_gate[:, expert_index]
        grad_act = jnp.einsum(
            "scd,fd->scf", grad_here, down_full[expert_index], preferred_element_type=jnp.float32
        )
        grad_gate = (
            grad_act
            * up_part[:, expert_index]
            * sigmoid_here
            * (1.0 + gate_here * (1.0 - sigmoid_here))
        )
        grad_up = grad_act * gate_here * sigmoid_here
        grad_before = jnp.concatenate([grad_gate, grad_up], axis=-1).astype(jnp.bfloat16)
        down_term = jnp.einsum(
            "scf,scd->fd", activated[:, expert_index], grad_here, preferred_element_type=jnp.float32
        )
        gate_up_term = jnp.einsum(
            "scd,scf->df", arrived[:, expert_index], grad_before, preferred_element_type=jnp.float32
        )
        row_grads.append(
            jnp.einsum(
                "scf,df->scd",
                grad_before,
                gate_up_full[expert_index],
                preferred_element_type=jnp.float32,
            ).astype(jnp.bfloat16)
        )
        shard_pair = (
            lax.psum_scatter(
                gate_up_term.astype(jnp.bfloat16), "wt", scatter_dimension=0, tiled=True
            ).astype(jnp.float32),
            lax.psum_scatter(
                down_term.astype(jnp.bfloat16), "wt", scatter_dimension=0, tiled=True
            ).astype(jnp.float32),
        )
        gate_up_grads.append(shard_pair[0])
        down_grads.append(shard_pair[1])
    row_back = lax.all_to_all(
        jnp.stack(row_grads, axis=1), "seq", split_axis=0, concat_axis=0, tiled=True
    ).reshape(expert_total * capacity, model_width)
    expert_gate_up_grad = jnp.stack(gate_up_grads, axis=0)
    expert_down_grad = jnp.stack(down_grads, axis=0)
    grad_hidden = jnp.sum(
        row_back[slots].reshape(token_rows, top_count, model_width).astype(jnp.float32), axis=1
    )
    inner_gate = jnp.sum(grad_gates * gate_values, axis=1, keepdims=True)
    grad_picked = (grad_gates - inner_gate) / picked_total
    route_match = routes[:, :, None] == jnp.arange(expert_total, dtype=jnp.int32)[None, None, :]
    grad_chances = jnp.sum(jnp.where(route_match, grad_picked[:, :, None], 0.0), axis=1)
    grad_logits = (
        chances * (grad_chances - jnp.sum(grad_chances * chances, axis=1, keepdims=True))
    ).astype(jnp.bfloat16)
    grad_hidden = grad_hidden + jnp.dot(
        grad_logits, router_full.T, preferred_element_type=jnp.float32
    )
    router_grad = jnp.dot(hidden_ffn.T, grad_logits, preferred_element_type=jnp.float32)
    ffn_gain_grad = jnp.sum(grad_hidden * normed_f, axis=0)
    grad_residual = grad_out + norm_back(grad_hidden * gain_ffn, normed_f, factor_f)
    grad_branch = grad_residual.astype(jnp.bfloat16)
    out_grad = jnp.dot(merged.T, grad_branch, preferred_element_type=jnp.float32)
    grad_merged = (
        jnp.dot(grad_branch, out_full.T, preferred_element_type=jnp.float32)
        .astype(jnp.bfloat16)
        .reshape(token_rows, H, HD)
    )
    grad_heads = jnp.swapaxes(
        lax.all_to_all(grad_merged, "seq", split_axis=1, concat_axis=0, tiled=True), 0, 1
    )

    def backward_head(operands):
        query_one, key_one, value_one, grad_one, log_one = operands

        def backward_block(carry, offset):
            key_acc, value_acc = carry
            query_block = lax.dynamic_slice_in_dim(query_one, offset, width, 0)
            segment_block = lax.dynamic_slice_in_dim(segments, offset, width, 0)
            grad_block = lax.dynamic_slice_in_dim(grad_one, offset, width, 0)
            log_block = lax.dynamic_slice_in_dim(log_one, offset, width, 0)
            logits = scores(query_block, key_one, segment_block, segments)
            weights = jnp.exp(logits - log_block[:, None])
            grad_weights = jnp.dot(grad_block, value_one.T, preferred_element_type=jnp.float32)
            inner = jnp.sum(weights * grad_weights, axis=-1, keepdims=True)
            grad_scores = (weights * (grad_weights - inner)).astype(jnp.bfloat16)
            factor = HD ** (-0.5)
            grad_query = jnp.dot(grad_scores, key_one, preferred_element_type=jnp.float32) * factor
            key_acc = (
                key_acc
                + jnp.dot(grad_scores.T, query_block, preferred_element_type=jnp.float32) * factor
            )
            value_acc = value_acc + jnp.dot(
                weights.astype(jnp.bfloat16).T, grad_block, preferred_element_type=jnp.float32
            )
            return ((key_acc, value_acc), grad_query.astype(jnp.bfloat16))

        zeros_acc = jnp.zeros((length, HD), jnp.float32)
        (key_acc, value_acc), grad_queries = lax.scan(
            backward_block, (zeros_acc, zeros_acc), offsets
        )
        return (
            grad_queries.reshape(length, HD),
            key_acc.astype(jnp.bfloat16),
            value_acc.astype(jnp.bfloat16),
        )

    grad_q_heads, grad_k_heads, grad_v_heads = lax.map(
        backward_head, (query_heads, key_heads, value_heads, grad_heads, log_totals)
    )
    grad_stack = jnp.swapaxes(jnp.stack([grad_q_heads, grad_k_heads, grad_v_heads]), 1, 2)
    grad_tokens = lax.all_to_all(grad_stack, "seq", split_axis=1, concat_axis=2, tiled=True).astype(
        jnp.float32
    )
    grad_q_normed = rotate(grad_tokens[0], positions, -1.0)
    grad_k_normed = rotate(grad_tokens[1], positions, -1.0)
    q_gain_grad = jnp.sum(grad_q_normed * normed_q, axis=(0, 1))
    k_gain_grad = jnp.sum(grad_k_normed * normed_k, axis=(0, 1))
    grad_q_raw = norm_back(grad_q_normed * gain_query, normed_q, factor_q)
    grad_k_raw = norm_back(grad_k_normed * gain_key, normed_k, factor_k)
    grad_projected = (
        jnp.stack([grad_q_raw, grad_k_raw, grad_tokens[2]], axis=1)
        .reshape(token_rows, 3 * H * HD)
        .astype(jnp.bfloat16)
    )
    qkv_grad = jnp.dot(hidden.T, grad_projected, preferred_element_type=jnp.float32)
    grad_normed_a = jnp.dot(grad_projected, qkv_full.T, preferred_element_type=jnp.float32)
    attn_gain_grad = jnp.sum(grad_normed_a * normed_a, axis=0)
    tokens_grad = grad_residual + norm_back(grad_normed_a * gain_attn, normed_a, factor_a)
    partial_sums = (
        lax.psum_scatter(
            qkv_grad.astype(jnp.bfloat16), "wt", scatter_dimension=0, tiled=True
        ).astype(jnp.float32),
        lax.psum_scatter(
            out_grad.astype(jnp.bfloat16), "wt", scatter_dimension=0, tiled=True
        ).astype(jnp.float32),
        lax.psum_scatter(
            router_grad.astype(jnp.bfloat16), "wt", scatter_dimension=0, tiled=True
        ).astype(jnp.float32),
        lax.psum_scatter(
            attn_gain_grad.astype(jnp.bfloat16), "wt", scatter_dimension=0, tiled=True
        ).astype(jnp.float32),
        lax.psum_scatter(
            ffn_gain_grad.astype(jnp.bfloat16), "wt", scatter_dimension=0, tiled=True
        ).astype(jnp.float32),
        lax.psum_scatter(
            q_gain_grad.astype(jnp.bfloat16), "wt", scatter_dimension=0, tiled=True
        ).astype(jnp.float32),
        lax.psum_scatter(
            k_gain_grad.astype(jnp.bfloat16), "wt", scatter_dimension=0, tiled=True
        ).astype(jnp.float32),
    )
    final = (
        lax.psum(partial_sums[0].astype(jnp.bfloat16), "seq").astype(jnp.float32),
        lax.psum(partial_sums[1].astype(jnp.bfloat16), "seq").astype(jnp.float32),
        lax.psum(partial_sums[2].astype(jnp.bfloat16), "seq").astype(jnp.float32),
        lax.psum(partial_sums[3].astype(jnp.bfloat16), "seq").astype(jnp.float32),
        lax.psum(partial_sums[4].astype(jnp.bfloat16), "seq").astype(jnp.float32),
        lax.psum(partial_sums[5].astype(jnp.bfloat16), "seq").astype(jnp.float32),
        lax.psum(partial_sums[6].astype(jnp.bfloat16), "seq").astype(jnp.float32),
    )
    return (
        output.astype(jnp.bfloat16)[None],
        tokens_grad[None],
        final[0],
        final[1],
        final[2],
        expert_gate_up_grad,
        expert_down_grad,
        final[3],
        final[4],
        final[5],
        final[6],
    )


def solution(mesh):
    in_specs = (
        P("wt", "seq", None),
        P("wt", "seq", None),
        P("wt", None),
        P("wt", "seq", None),
        P("wt", None),
        P("wt", None),
        P("wt", None),
        P("seq", "wt", None),
        P("seq", "wt", None),
        P("wt"),
        P("wt"),
        P("wt"),
        P("wt"),
    )
    out_specs = (
        P("wt", "seq", None),
        P("wt", "seq", None),
        P("wt", None),
        P("wt", None),
        P("wt", None),
        P("seq", "wt", None),
        P("seq", "wt", None),
        P("wt"),
        P("wt"),
        P("wt"),
        P("wt"),
    )
    return jax.shard_map(body, mesh=mesh, in_specs=in_specs, out_specs=out_specs, check_vma=False)
```

profile of v0, /device:TPU:0, one launch (start us, length us, event | category | flops | bytes accessed | tf_op | source)
XLA Modules:
  0.0 2038.2 jit_solution(6947231434225680850)
XLA Ops:
  11.2 15.2 all-reduce.7
  35.8 102.1 %all-gather.7.cloned.1.call-done = bf16[2048,6144]{1,0:T(8,128)(2,1)} async-done(((bf16[256,6144]{1,0:T(8,128)(2,1)}), bf16[2048,6144]{1,0:T(8,128)(2,1)}) %all-gather.7.cloned.1.call-update) | async-done | bytes 25165840 | tf_op jit(solution)/shard_map/all_gather | solution.py:62
  137.9 30.7 %copy.134 = bf16[6144,2048]{1,0:T(8,128)(2,1)} copy(bf16[6144,2048]{0,1:T(8,128)(2,1)} %bitcast.536) | data formatting | bytes 50331648 | tf_op jit(solution)/shard_map/dot_general | solution.py:91
  205.7 22.4 %all-to-all-done = bf16[3,128,16,128]{1,3,0,2:T(8,128)(2,1)S(1)} async-done(((bf16[3,128,16,128]{1,3,0,2:T(8,128)(2,1)}), bf16[3,128,16,128]{1,3,0,2:T(8,128)(2,1)S(1)}, u32[]{:S(2)}, u32[]{:S(2)}) %all-to-all-start) | async-done | bytes 1572896 | tf_op jit(solution)/shard_map/all_to_all | solution.py:99
  340.9 132.4 %all-to-all-done.2 = bf16[4,4,128,2048]{3,2,1,0:T(8,128)(2,1)} async-done(((bf16[4,4,128,2048]{3,2,1,0:T(8,128)(2,1)}), bf16[4,4,128,2048]{3,2,1,0:T(8,128)(2,1)}, u32[]{:S(2)}, u32[]{:S(2)}) %all-to-all-start.2) | async-done | bytes 8388640 | tf_op jit(solution)/shard_map/all_to_all | solution.py:157
  479.1 26.3 %fusion.56 = f32[4,4,128,2048]{3,2,0,1:T(8,128)} fusion(bf16[4,2048,2048]{2,1,0:T(8,128)(2,1)} %all-gather.11.cloned.1.call-done, bf16[4,4,128,2048]{3,2,1,0:T(8,128)(2,1)} %all-to-all-done.2), kind=kOutput, calls=%fused_computation.99 | convolution fusion | flops 17179869184 | bytes 58720256 | tf_op jit(solution)/shard_map/secd,edf->secf/dot_general | solution.py:164
  515.5 17.4 convert_bitcast_fusion
  541.2 120.5 %all-to-all-done.4 = bf16[4,4,128,2048]{3,2,1,0:T(8,128)(2,1)} async-done(((bf16[4,4,128,2048]{3,2,1,0:T(8,128)(2,1)}), bf16[4,4,128,2048]{3,2,1,0:T(8,128)(2,1)}, u32[]{:S(2)}, u32[]{:S(2)}) %all-to-all-start.4) | async-done | bytes 8388640 | tf_op jit(solution)/shard_map/all_to_all | solution.py:185
  741.6 108.7 %all-to-all-done.3 = bf16[4,4,128,2048]{3,2,1,0:T(8,128)(2,1)} async-done(((bf16[4,4,128,2048]{3,2,1,0:T(8,128)(2,1)}), bf16[4,4,128,2048]{3,2,1,0:T(8,128)(2,1)}, u32[]{:S(2)}, u32[]{:S(2)}) %all-to-all-start.3) | async-done | bytes 8388640 | tf_op jit(solution)/shard_map/all_to_all | solution.py:174
  874.8 163.8 %all-to-all-done.5 = bf16[4,4,128,2048]{3,2,1,0:T(8,128)(2,1)} async-done(((bf16[4,4,128,2048]{3,2,1,0:T(8,128)(2,1)}), bf16[4,4,128,2048]{3,2,1,0:T(8,128)(2,1)}, u32[]{:S(2)}, u32[]{:S(2)}) %all-to-all-start.5) | async-done | bytes 8388640 | tf_op jit(solution)/shard_map/all_to_all | solution.py:234
  1084.8 15.4 while.27
  1102.6 39.7 %all_to_all.77 = bf16[3,512,4,128]{3,2,0,1:T(4,128)(2,1)} all-to-all(bf16[3,512,4,128]{3,2,0,1:T(4,128)(2,1)S(1)} %maximum_bitcast_fusion), channel_id=1, replica_groups=mesh['seq'=4,'wt'=8] {'seq'}, dimensions={1} | all-to-all | bytes 3145728 | tf_op jit(solution)/shard_map/all_to_all | solution.py:305
  1234.8 80.2 %reduce-scatter.12.cloned.1.call-done = bf16[256,6144]{1,0:T(8,128)(2,1)} async-done(((bf16[2048,6144]{1,0:T(8,128)(2,1)}), bf16[256,6144]{1,0:T(8,128)(2,1)}) %reduce-scatter.12.cloned.1.call-update) | async-done | bytes 3145744 | tf_op jit(solution)/shard_map/reduce_scatter | solution.py:324
  1316.3 53.8 %reduce-scatter.32.cloned.1.call-done = bf16[128,2048]{1,0:T(8,128)(2,1)} async-done(((bf16[1024,2048]{1,0:T(8,128)(2,1)}), bf16[128,2048]{1,0:T(8,128)(2,1)}) %reduce-scatter.32.cloned.1.call-update) | async-done | bytes 524304 | tf_op jit(solution)/shard_map/reduce_scatter | solution.py:228
  1370.1 54.5 %reduce-scatter.30.cloned.1.call-done = bf16[128,2048]{1,0:T(8,128)(2,1)} async-done(((bf16[1024,2048]{1,0:T(8,128)(2,1)}), bf16[128,2048]{1,0:T(8,128)(2,1)}) %reduce-scatter.30.cloned.1.call-update) | async-done | bytes 524304 | tf_op jit(solution)/shard_map/reduce_scatter | solution.py:228
  1424.7 54.6 %reduce-scatter.26.cloned.1.call-done = bf16[128,2048]{1,0:T(8,128)(2,1)} async-done(((bf16[1024,2048]{1,0:T(8,128)(2,1)}), bf16[128,2048]{1,0:T(8,128)(2,1)}) %reduce-scatter.26.cloned.1.call-update) | async-done | bytes 524304 | tf_op jit(solution)/shard_map/reduce_scatter | solution.py:228
  1479.2 54.4 %reduce-scatter.28.cloned.1.call-done = bf16[128,2048]{1,0:T(8,128)(2,1)} async-done(((bf16[1024,2048]{1,0:T(8,128)(2,1)}), bf16[128,2048]{1,0:T(8,128)(2,1)}) %reduce-scatter.28.cloned.1.call-update) | async-done | bytes 524304 | tf_op jit(solution)/shard_map/reduce_scatter | solution.py:228
  1537.5 71.1 %reduce-scatter.20.cloned.1.call-done = bf16[256,2048]{1,0:T(8,128)(2,1)} async-done(((bf16[2048,2048]{1,0:T(8,128)(2,1)}), bf16[256,2048]{1,0:T(8,128)(2,1)}) %reduce-scatter.20.cloned.1.call-update) | async-done | bytes 1048592 | tf_op jit(solution)/shard_map/reduce_scatter | solution.py:225
  1608.6 74.8 %reduce-scatter.22.cloned.1.call-done = bf16[256,2048]{1,0:T(8,128)(2,1)} async-done(((bf16[2048,2048]{1,0:T(8,128)(2,1)}), bf16[256,2048]{1,0:T(8,128)(2,1)}) %reduce-scatter.22.cloned.1.call-update) | async-done | bytes 1048592 | tf_op jit(solution)/shard_map/reduce_scatter | solution.py:225
  1683.5 75.0 %reduce-scatter.18.cloned.1.call-done = bf16[256,2048]{1,0:T(8,128)(2,1)} async-done(((bf16[2048,2048]{1,0:T(8,128)(2,1)}), bf16[256,2048]{1,0:T(8,128)(2,1)}) %reduce-scatter.18.cloned.1.call-update) | async-done | bytes 1048592 | tf_op jit(solution)/shard_map/reduce_scatter | solution.py:225
  1758.5 74.8 %reduce-scatter.24.cloned.1.call-done = bf16[256,2048]{1,0:T(8,128)(2,1)} async-done(((bf16[2048,2048]{1,0:T(8,128)(2,1)}), bf16[256,2048]{1,0:T(8,128)(2,1)}) %reduce-scatter.24.cloned.1.call-update) | async-done | bytes 1048592 | tf_op jit(solution)/shard_map/reduce_scatter | solution.py:225
  1838.6 14.6 fusion.102
  1867.6 19.9 all-reduce.8
  1893.2 131.9 %all-reduce.12.cloned.1.call-done = (bf16[256,6144]{1,0:T(8,128)(2,1)}, bf16[256,2048]{1,0:T(8,128)(2,1)}) async-done(((bf16[256,6144]{1,0:T(8,128)(2,1)}, bf16[256,2048]{1,0:T(8,128)(2,1)}), (bf16[256,6144]{1,0:T(8,128)(2,1)}, bf16[256,2048]{1,0:T(8,128)(2,1)})) %all-reduce.12.cloned.1.call-update) | async-done | bytes 4194320 | tf_op jit(solution)/shard_map/psum | solution.py:347
  (398 shorter events, 490.4 us)
Async XLA Ops:
  7.2 130.7 %all-gather.7.cloned.1.call-start = ((), (), s32[]{:S(2)}) async-start(), calls=%async_computation.19 | async-start | bytes 28311552 | tf_op jit(solution)/shard_map/all_gather | solution.py:62
  8.0 251.5 %all-gather.9.cloned.1.call-start = ((), (), s32[]{:S(2)}) async-start(), calls=%async_computation.20 | async-start | bytes 9437184 | tf_op jit(solution)/shard_map/all_gather | solution.py:63
  8.7 470.3 %all-gather.11.cloned.1.call-start = ((), (), s32[]{:S(2)}) async-start(), calls=%async_computation.21 | async-start | bytes 37748736 | tf_op jit(solution)/shard_map/all_gather | solution.py:152
  26.5 154.4 %copy-start.57 = (f32[128]{0:T(128)}, f32[128]{0:T(128)S(1)}, u32[]{:S(2)}) copy-start(f32[128]{0:T(128)S(1)} %convert_element_type.260) | copy-start | bytes 1540
  183.8 44.4 %all-to-all-start = ((bf16[3,128,16,128]{1,3,0,2:T(8,128)(2,1)}), bf16[3,128,16,128]{1,3,0,2:T(8,128)(2,1)S(1)}, u32[]{:S(2)}, u32[]{:S(2)}) async-start(bf16[3,128,16,128]{1,3,0,2:T(8,128)(2,1)} %copy.135), calls=%async_computation | async-start | bytes 3145728 | tf_op jit(solution)/shard_map/all_to_all | solution.py:99
  190.7 324.8 %all-gather.13.cloned.1.call-start = ((), (), s32[]{:S(2)}) async-start(), calls=%async_computation.22 | async-start | bytes 18874368 | tf_op jit(solution)/shard_map/all_gather | solution.py:153
  241.5 17.6 all-to-all-start.1
  285.7 187.7 %all-to-all-start.2 = ((bf16[4,4,128,2048]{3,2,1,0:T(8,128)(2,1)}), bf16[4,4,128,2048]{3,2,1,0:T(8,128)(2,1)}, u32[]{:S(2)}, u32[]{:S(2)}) async-start(bf16[4,4,128,2048]{3,2,1,0:T(8,128)(2,1)} %broadcast_select_fusion), calls=%async_computation.2 | async-start | bytes 16777216 | tf_op jit(solution)/shard_map/all_to_all | solution.py:157
  473.4 188.3 %all-to-all-start.4 = ((bf16[4,4,128,2048]{3,2,1,0:T(8,128)(2,1)}), bf16[4,4,128,2048]{3,2,1,0:T(8,128)(2,1)}, u32[]{:S(2)}, u32[]{:S(2)}) async-start(bf16[4,4,128,2048]{3,2,1,0:T(8,128)(2,1)} %select_convert_fusion), calls=%async_computation.4 | async-start | bytes 16777216 | tf_op jit(solution)/shard_map/all_to_all | solution.py:185
  661.7 188.6 %all-to-all-start.3 = ((bf16[4,4,128,2048]{3,2,1,0:T(8,128)(2,1)}), bf16[4,4,128,2048]{3,2,1,0:T(8,128)(2,1)}, u32[]{:S(2)}, u32[]{:S(2)}) async-start(bf16[4,4,128,2048]{3,2,1,0:T(8,128)(2,1)} %copy.150), calls=%async_computation.3 | async-start | bytes 16777216 | tf_op jit(solution)/shard_map/all_to_all | solution.py:174
  850.3 188.3 %all-to-all-start.5 = ((bf16[4,4,128,2048]{3,2,1,0:T(8,128)(2,1)}), bf16[4,4,128,2048]{3,2,1,0:T(8,128)(2,1)}, u32[]{:S(2)}, u32[]{:S(2)}) async-start(bf16[4,4,128,2048]{3,2,1,0:T(8,128)(2,1)} %copy.155), calls=%async_computation.5 | async-start | bytes 16777216 | tf_op jit(solution)/shard_map/all_to_all | solution.py:234
  1067.0 17.5 all-to-all-start.6
  1070.5 164.4 %reduce-scatter.14.cloned.1.call-start = ((), (), s32[]{:S(2)}) async-start(), calls=%async_computation.24 | async-start | bytes 9437184 | tf_op jit(solution)/shard_map/reduce_scatter | solution.py:327
  1076.3 238.7 %reduce-scatter.12.cloned.1.call-start = ((), (), s32[]{:S(2)}) async-start(), calls=%async_computation.23 | async-start | bytes 28311552 | tf_op jit(solution)/shard_map/reduce_scatter | solution.py:324
  1161.0 209.2 %reduce-scatter.32.cloned.1.call-start = ((), (), s32[]{:S(2)}) async-start(), calls=%async_computation.33 | async-start | bytes 4718592 | tf_op jit(solution)/shard_map/reduce_scatter | solution.py:228
  1167.6 257.1 %reduce-scatter.30.cloned.1.call-start = ((), (), s32[]{:S(2)}) async-start(), calls=%async_computation.32 | async-start | bytes 4718592 | tf_op jit(solution)/shard_map/reduce_scatter | solution.py:228
  1175.5 303.7 %reduce-scatter.26.cloned.1.call-start = ((), (), s32[]{:S(2)}) async-start(), calls=%async_computation.30 | async-start | bytes 4718592 | tf_op jit(solution)/shard_map/reduce_scatter | solution.py:228
  1183.3 350.3 %reduce-scatter.28.cloned.1.call-start = ((), (), s32[]{:S(2)}) async-start(), calls=%async_computation.31 | async-start | bytes 4718592 | tf_op jit(solution)/shard_map/reduce_scatter | solution.py:228
  1190.6 418.0 %reduce-scatter.20.cloned.1.call-start = ((), (), s32[]{:S(2)}) async-start(), calls=%async_computation.27 | async-start | bytes 9437184 | tf_op jit(solution)/shard_map/reduce_scatter | solution.py:225
  1201.8 481.7 %reduce-scatter.22.cloned.1.call-start = ((), (), s32[]{:S(2)}) async-start(), calls=%async_computation.28 | async-start | bytes 9437184 | tf_op jit(solution)/shard_map/reduce_scatter | solution.py:225
  1211.9 546.6 %reduce-scatter.18.cloned.1.call-start = ((), (), s32[]{:S(2)}) async-start(), calls=%async_computation.26 | async-start | bytes 9437184 | tf_op jit(solution)/shard_map/reduce_scatter | solution.py:225
  1222.5 610.8 %reduce-scatter.24.cloned.1.call-start = ((), (), s32[]{:S(2)}) async-start(), calls=%async_computation.29 | async-start | bytes 9437184 | tf_op jit(solution)/shard_map/reduce_scatter | solution.py:225
  1232.7 634.9 %reduce-scatter.16.cloned.1.call-start = ((), (), s32[]{:S(2)}) async-start(), calls=%async_computation.25 | async-start | bytes 73728 | tf_op jit(solution)/shard_map/reduce_scatter | solution.py:330
  1234.5 790.5 %all-reduce.12.cloned.1.call-start = ((), (), s32[]{:S(2)}) async-start(), calls=%async_computation.34 | async-start | bytes 8388608 | tf_op jit(solution)/shard_map/psum | solution.py:347
  (73 other events, 1759.3 us)
Sparse Core Ops, SparseCore 0:
  9.9 127.9 all-gather.6
  139.8 54.2 all-gather.8
  196.0 160.8 all-gather.10
  358.6 89.7 all-gather.12
  1076.4 71.3 reduce-scatter.13
  1161.1 153.8 reduce-scatter.11
  1318.9 51.1 reduce-scatter.31
  1373.5 51.1 reduce-scatter.29
  1428.0 51.1 reduce-scatter.25
  1482.4 51.1 reduce-scatter.27
  1537.1 71.5 reduce-scatter.19
  1612.0 71.4 reduce-scatter.21
  1686.9 71.4 reduce-scatter.17
  1761.8 71.4 reduce-scatter.23
  1836.2 31.4 reduce-scatter.15
  1869.9 155.1 all-reduce.11
where the time goes:
time: 2050 us; the launch traced here: 2040 us
  waiting for transfers between devices  1390 us (68%)
  matrix products  249 us (12%)
  local copies, waits for them, and re-layouts  149 us (7%)
  blocking collectives  114 us (6%)
  other arithmetic  77.4 us (4%)
  starting transfers between devices  38.6 us (2%)
    reduce_scatter x4, waiting for transfers between devices, body(): lax.psum_scatter(gate_up_term.astype(jnp.bfloat16), 'wt', scatter_dimensi...  296 us
    reduce_scatter x4, waiting for transfers between devices, body(): lax.psum_scatter(down_term.astype(jnp.bfloat16), 'wt', scatter_dimension=...  217 us
    all_to_all x1, waiting for transfers between devices, body(): lax.all_to_all(jnp.stack(row_grads, axis=1), 'seq', split_axis=0, concat_...  164 us
    all_to_all x1, waiting for transfers between devices, body(): lax.all_to_all(sent_rows.reshape(seq_total, local_experts, capacity, mode...  132 us
    psum x1, waiting for transfers between devices, body(): lax.psum(partial_sums[0].astype(jnp.bfloat16), 'seq').astype(jnp.float32)  132 us
    all_to_all x1, waiting for transfers between devices, body(): lax.all_to_all(slot_grads.reshape(seq_total, local_experts, capacity, mod...  120 us
    all_to_all x1, waiting for transfers between devices, body(): lax.all_to_all(expert_out, 'seq', split_axis=0, concat_axis=0, tiled=True)  109 us
    all_gather x1, waiting for transfers between devices, body(): lax.all_gather(w_qkv, 'wt', axis=0, tiled=True)  102 us
  transfers between devices with their start and end apart: 23, of which 19 were waited for; matrix products, arithmetic and copies ran while one was open for 21% of the time, Pallas kernels for 0%

commit v1 on v0

v1 whole, which is shorter than its diff:
```python
import jax
import jax.numpy as jnp
import numpy as np
from jax import lax
from jax.sharding import PartitionSpec as P

H = 16
HD = 128
FF = 1024

EPS = 1e-06
THETA = 50000.0
NEG = -1e30
LANES = 128
BF = jnp.bfloat16
F32 = jnp.float32


def normalize(values):
    factor = lax.rsqrt(jnp.mean(values * values, axis=-1, keepdims=True) + EPS)
    return (values * factor, factor)


def norm_back(grad_normed, normed_values, factor):
    return factor * (
        grad_normed - normed_values * jnp.mean(grad_normed * normed_values, axis=-1, keepdims=True)
    )


def rope_tables(length):
    half = HD // 2
    freq = THETA ** (-jnp.arange(half, dtype=F32) * 2.0 / HD)
    angle = jnp.arange(length, dtype=F32)[:, None] * freq[None, :]
    return jnp.cos(angle)[:, None, :], jnp.sin(angle)[:, None, :]


def rotate(values, cosine, sine):
    half = values.shape[-1] // 2
    first = values[..., :half]
    second = values[..., half:]
    return jnp.concatenate(
        [first * cosine - second * sine, second * cosine + first * sine], axis=-1
    )


def dot(left, right, dims):
    return lax.dot_general(left, right, (dims, ((), ())), preferred_element_type=F32)


def nn(left, right):
    return dot(left, right, ((1,), (0,)))


def nt(left, right):
    return dot(left, right, ((1,), (1,)))


def tn(left, right):
    return dot(left, right, ((0,), (0,)))


def split_two(values):
    high = values.astype(BF)
    low = (values - high.astype(F32)).astype(BF)
    return high, low


def body(
    tokens,
    cotangent,
    segment_ids,
    expert_routes,
    w_qkv,
    w_out,
    w_router,
    w_gate_up,
    w_down,
    attn_gain,
    ffn_gain,
    q_gain,
    k_gain,
):
    seq_total = lax.axis_size("seq")
    wt_total = lax.axis_size("wt")
    seq_me = lax.axis_index("seq")
    rows = tokens.shape[1]
    model = tokens.shape[2]
    length = rows * seq_total
    shard = w_qkv.shape[0]
    local_experts = w_gate_up.shape[0]
    experts = w_router.shape[1]
    heads = H // seq_total
    cols = 3 * heads * HD
    gain_part = q_gain.shape[0]

    tokens_all = lax.all_gather(tokens[0], "seq", axis=0, tiled=True)
    routes_all = lax.all_gather(expert_routes[0], "seq", axis=0, tiled=True)
    w_here = lax.dynamic_slice_in_dim(
        w_qkv.reshape(shard, 3, seq_total, heads * HD), seq_me, 1, axis=2
    ).reshape(shard, cols)
    small = jnp.concatenate(
        [
            w_router,
            attn_gain[:, None],
            ffn_gain[:, None],
            jnp.pad(q_gain, (0, shard - gain_part))[:, None],
            jnp.pad(k_gain, (0, shard - gain_part))[:, None],
        ],
        axis=1,
    )
    small = jnp.pad(small, ((0, 0), (0, LANES - small.shape[1])))
    qkv_full = lax.all_gather(jnp.concatenate([w_here, small], axis=1), "wt", axis=0, tiled=True)
    out_full = lax.all_gather(w_out, "wt", axis=0, tiled=True)
    grad_all = lax.all_gather(cotangent[0], "seq", axis=0, tiled=True)
    expert_full = [
        lax.all_gather(jnp.concatenate([w_gate_up[e], w_down[e]], axis=0), "wt", axis=0)
        for e in range(local_experts)
    ]

    small_full = qkv_full[:, cols:]
    router_full = small_full[:, :experts]
    picker = np.zeros((8, LANES), np.float32)
    for row in range(4):
        picker[row, experts + row] = 1.0
    gain_rows = nt(jnp.asarray(picker, BF), small_full)
    gain_attn = gain_rows[0]
    gain_ffn = gain_rows[1]
    gain_query = gain_rows[2].reshape(wt_total, shard)[:, :gain_part].reshape(HD)
    gain_key = gain_rows[3].reshape(wt_total, shard)[:, :gain_part].reshape(HD)

    segments = segment_ids[0]
    same = segments[:, None] == segments[None, :]
    cosine, sine = rope_tables(length)
    normed_all, _ = normalize(tokens_all.astype(F32))
    hidden = (normed_all * gain_attn).astype(BF)
    projected = nn(hidden, qkv_full)[:, :cols].reshape(length, 3, heads, HD)
    normed_q, factor_q = normalize(projected[:, 0])
    normed_k, factor_k = normalize(projected[:, 1])
    queries = jnp.swapaxes(rotate(normed_q * gain_query, cosine, sine).astype(BF), 0, 1)
    keys = jnp.swapaxes(rotate(normed_k * gain_key, cosine, sine).astype(BF), 0, 1)
    values = jnp.swapaxes(projected[:, 2].astype(BF), 0, 1)
    scale = HD ** (-0.5)

    def bmm(left, right, dims):
        return lax.dot_general(left, right, (dims, ((0,), (0,))), preferred_element_type=F32)

    logits = jnp.where(same[None], bmm(queries, keys, ((2,), (2,))) * scale, NEG)
    powers = jnp.exp(logits - jnp.max(logits, axis=-1, keepdims=True))
    weights = powers / jnp.sum(powers, axis=-1, keepdims=True)
    weights_low = weights.astype(BF)
    attended = bmm(weights_low, values, ((2,), (1,))).astype(BF)
    merged = lax.all_to_all(
        jnp.swapaxes(attended, 0, 1), "seq", split_axis=0, concat_axis=1, tiled=True
    ).reshape(rows, H * HD)

    inputs = tokens[0].astype(F32)
    residual = inputs + nn(merged, out_full)
    normed_f, factor_f = normalize(residual)
    hidden_own = (normed_f * gain_ffn).astype(BF)
    hidden_ffn = lax.all_gather(hidden_own, "seq", axis=0, tiled=True)

    chances = jax.nn.softmax(nn(hidden_ffn, router_full), axis=-1)
    expert_ids = jnp.arange(experts, dtype=jnp.int32)
    routed = jnp.any(routes_all[:, :, None] == expert_ids[None, None, :], axis=1)
    picked = jnp.where(routed, chances, 0.0)
    picked_total = jnp.sum(picked, axis=1, keepdims=True)
    gates = picked / picked_total
    gates_here = lax.dynamic_slice_in_dim(gates, seq_me * local_experts, local_experts, axis=1)

    out_part = jnp.zeros((length, model), F32)
    grad_hidden_part = jnp.zeros((length, model), F32)
    gate_grads = []
    expert_grads = []
    for e in range(local_experts):
        gate = gates_here[:, e : e + 1]
        gate_up = expert_full[e][:, : model // wt_total].reshape(model, 2 * FF)
        down = expert_full[e][:, model // wt_total :].reshape(FF, model)
        before = nn(hidden_ffn, gate_up)
        gate_part = before[:, :FF]
        up_part = before[:, FF:]
        sigmoid_gate = jax.nn.sigmoid(gate_part)
        silu_gate = gate_part * sigmoid_gate
        activated = silu_gate * up_part
        scaled = (gate * activated).astype(BF)
        grad_act = nt(grad_all, down)
        gate_grads.append(jnp.sum(grad_act * activated, axis=1, keepdims=True))
        grad_act = grad_act * gate
        grad_gate = grad_act * up_part * sigmoid_gate * (1.0 + gate_part * (1.0 - sigmoid_gate))
        grad_up = grad_act * silu_gate
        grad_before = jnp.concatenate([grad_gate, grad_up], axis=-1).astype(BF)
        out_part = out_part + nn(scaled, down)
        grad_hidden_part = grad_hidden_part + nt(grad_before, gate_up)
        gate_up_grad = tn(hidden_ffn, grad_before).astype(BF)
        down_grad = tn(scaled, grad_all).astype(BF)
        joined = jnp.concatenate(
            [
                gate_up_grad.reshape(wt_total, model // wt_total, 2 * FF),
                down_grad.reshape(wt_total, FF // wt_total, model),
            ],
            axis=1,
        )
        expert_grads.append(
            lax.psum_scatter(joined, "wt", scatter_dimension=0, tiled=False).astype(F32)
        )
    gate_up_out = jnp.stack([g[: model // wt_total] for g in expert_grads])
    down_out = jnp.stack([g[model // wt_total :] for g in expert_grads])

    gate_grad_part = jnp.concatenate(gate_grads, axis=1)
    gate_high, gate_low = split_two(gate_grad_part)

    def spread(part):
        wide = jnp.zeros((length, experts), BF)
        return lax.dynamic_update_slice(wide, part, (0, seq_me * local_experts))

    returned = lax.psum_scatter(
        jnp.concatenate(
            [grad_hidden_part.astype(BF), spread(gate_high), spread(gate_low)], axis=1
        ),
        "seq",
        scatter_dimension=0,
        tiled=True,
    ).astype(F32)
    grad_hidden = returned[:, :model]
    gate_grad = returned[:, model : model + experts] + returned[:, model + experts :]
    moe_out = lax.psum_scatter(
        out_part.astype(BF), "seq", scatter_dimension=0, tiled=True
    ).astype(F32)
    output = (residual + moe_out).astype(BF)

    def own(full):
        return lax.dynamic_slice_in_dim(full, seq_me * rows, rows, axis=0)

    chances_own = own(chances)
    routed_own = own(routed)
    gates_own = own(gates)
    inner_gate = jnp.sum(gate_grad * gates_own, axis=1, keepdims=True)
    grad_chances = jnp.where(routed_own, (gate_grad - inner_gate) / own(picked_total), 0.0)
    grad_logits = (
        chances_own
        * (grad_chances - jnp.sum(grad_chances * chances_own, axis=1, keepdims=True))
    ).astype(BF)
    grad_hidden = grad_hidden + nt(grad_logits, router_full)
    router_grad = tn(hidden_own, grad_logits)
    ffn_gain_grad = jnp.sum(grad_hidden * normed_f, axis=0)
    grad_residual = cotangent[0].astype(F32) + norm_back(
        grad_hidden * gain_ffn, normed_f, factor_f
    )
    grad_branch = grad_residual.astype(BF)
    grad_merged = nt(grad_branch, out_full).astype(BF).reshape(rows, H, HD)
    grad_heads = jnp.swapaxes(
        lax.all_to_all(grad_merged, "seq", split_axis=1, concat_axis=0, tiled=True), 0, 1
    )
    out_grad = lax.psum_scatter(
        tn(merged, grad_branch).astype(BF), "wt", scatter_dimension=0, tiled=True
    )
    out_grad = lax.psum(out_grad, "seq").astype(F32)

    grad_weights = bmm(grad_heads, values, ((2,), (2,)))
    inner = jnp.sum(weights * grad_weights, axis=-1, keepdims=True)
    grad_scores = (weights * (grad_weights - inner)).astype(BF)
    grad_q = jnp.swapaxes(bmm(grad_scores, keys, ((2,), (1,))), 0, 1) * scale
    grad_k = jnp.swapaxes(bmm(grad_scores, queries, ((1,), (1,))), 0, 1) * scale
    grad_v = jnp.swapaxes(bmm(weights_low, grad_heads, ((1,), (1,))), 0, 1)
    grad_q_normed = rotate(grad_q, cosine, -sine)
    grad_k_normed = rotate(grad_k, cosine, -sine)
    q_gain_grad = jnp.sum(grad_q_normed * normed_q, axis=(0, 1))
    k_gain_grad = jnp.sum(grad_k_normed * normed_k, axis=(0, 1))
    grad_q_raw = norm_back(grad_q_normed * gain_query, normed_q, factor_q)
    grad_k_raw = norm_back(grad_k_normed * gain_key, normed_k, factor_k)
    grad_projected = (
        jnp.stack([grad_q_raw, grad_k_raw, grad_v], axis=1).reshape(length, cols).astype(BF)
    )
    qkv_grad = tn(hidden, grad_projected)
    grad_normed_part = nt(
        jnp.pad(grad_projected, ((0, 0), (0, LANES))), qkv_full
    )
    attn_gain_grad = jnp.sum(grad_normed_part * normed_all, axis=0)
    grad_normed_own = lax.psum_scatter(
        grad_normed_part.astype(BF), "seq", scatter_dimension=0, tiled=True
    ).astype(F32)
    normed_a, factor_a = normalize(inputs)
    tokens_grad = grad_residual + norm_back(grad_normed_own * gain_attn, normed_a, factor_a)

    def gain_column(vector):
        return jnp.pad(
            vector.reshape(wt_total, gain_part), ((0, 0), (0, shard - gain_part))
        ).reshape(model, 1)

    small_grad = jnp.concatenate(
        [
            router_grad,
            attn_gain_grad[:, None],
            ffn_gain_grad[:, None],
            gain_column(q_gain_grad),
            gain_column(k_gain_grad),
        ],
        axis=1,
    )
    small_grad = jnp.pad(small_grad, ((0, 0), (0, LANES - small_grad.shape[1])))
    scattered = lax.psum_scatter(
        jnp.concatenate([qkv_grad, small_grad], axis=1).astype(BF),
        "wt",
        scatter_dimension=0,
        tiled=True,
    )
    collected = lax.all_gather(scattered, "seq", axis=0).astype(F32)
    qkv_out = (
        collected[:, :, :cols]
        .reshape(seq_total, shard, 3, heads * HD)
        .transpose(1, 2, 0, 3)
        .reshape(shard, 3 * H * HD)
    )
    small_out = jnp.sum(collected[:, :, cols:], axis=0)
    return (
        output[None],
        tokens_grad[None],
        qkv_out,
        out_grad,
        small_out[:, :experts],
        gate_up_out,
        down_out,
        small_out[:, experts],
        small_out[:, experts + 1],
        small_out[:gain_part, experts + 2],
        small_out[:gain_part, experts + 3],
    )


def solution(mesh):
    in_specs = (
        P("wt", "seq", None),
        P("wt", "seq", None),
        P("wt", None),
        P("wt", "seq", None),
        P("wt", None),
        P("wt", None),
        P("wt", None),
        P("seq", "wt", None),
        P("seq", "wt", None),
        P("wt"),
        P("wt"),
        P("wt"),
        P("wt"),
    )
    out_specs = (
        P("wt", "seq", None),
        P("wt", "seq", None),
        P("wt", None),
        P("wt", None),
        P("wt", None),
        P("seq", "wt", None),
        P("seq", "wt", None),
        P("wt"),
        P("wt"),
        P("wt"),
        P("wt"),
    )
    return jax.shard_map(body, mesh=mesh, in_specs=in_specs, out_specs=out_specs, check_vma=False)
```

time: 2050 us -> 1470 us (0.72)
  waiting for transfers between devices: 1390 us -> 968 us
  blocking collectives: 114 us -> 44.8 us
  matrix products: 249 us -> 200 us
  starting transfers between devices: 38.6 us -> 5.5 us
    all_to_all x6 -> x0, waiting for transfers between devices: 553 us -> none  [the longest x1 164 us: body(): lax.all_to_all(jnp.stack(row_grads, axis=1), 'seq', split_axis=0, concat_...]
    all_gather x4 -> x10, waiting for transfers between devices: 102 us -> 421 us  [the longest x4 249 us: body(): lax.all_gather(jnp.concatenate([w_gate_up[e], w_down[e]], axis=0), 'wt',...]
    reduce_scatter x11 -> x9, waiting for transfers between devices: 594 us -> 480 us  [the longest x4 369 us: body(): lax.psum_scatter(joined, 'wt', scatter_dimension=0, tiled=False).astype(F32)]
    psum x1, waiting for transfers between devices: 132 us -> 49.6 us  [body(): out_grad = lax.psum(out_grad, 'seq').astype(F32)]
    slice x8 -> x25, local copies, waits for them, and re-layouts: 3.32 us -> 76.2 us  [the longest x4 33.4 us: body(): gate_up = expert_full[e][:, :model // wt_total].reshape(model, 2 * FF)]
    gather x9 -> x0, local copies, waits for them, and re-layouts: 66.3 us -> none  [the longest x1 13.7 us: body(): row_back[slots].reshape(token_rows, top_count, model_width)]
    dot_general x55 -> x39, matrix products: 249 us -> 196 us  [the longest x34 188 us: dot(): lax.dot_general(left, right, (dims, ((), ())), preferred_element_type=F32)]
    concatenate x0 -> x10, other arithmetic: none -> 52.5 us  [the longest x4 36.3 us: body(): jnp.concatenate([gate_up_grad.reshape(wt_total, model // wt_total, 2 * FF...]
  transfers between devices with their start and end apart: 23 -> 21, of which waited for: 19 -> 19; matrix products, arithmetic and copies ran while one was open for 21% -> 20% of each run, Pallas kernels for 0% -> 0%
where the time goes in v1:
time: 1470 us; the launch traced here: 1460 us
  waiting for transfers between devices  968 us (66%)
  matrix products  200 us (14%)
  local copies, waits for them, and re-layouts  134 us (9%)
  other arithmetic  88.6 us (6%)
  blocking collectives  44.8 us (3%)
  between operations  16 us (1%)
    reduce_scatter x4, waiting for transfers between devices, body(): lax.psum_scatter(joined, 'wt', scatter_dimension=0, tiled=False).astype(F32)  369 us
    all_gather x4, waiting for transfers between devices, body(): lax.all_gather(jnp.concatenate([w_gate_up[e], w_down[e]], axis=0), 'wt',...  249 us
    dot_general x34, matrix products, dot(): lax.dot_general(left, right, (dims, ((), ())), preferred_element_type=F32)  188 us
    all_gather x1, waiting for transfers between devices, body(): collected = lax.all_gather(scattered, 'seq', axis=0).astype(F32)  59.4 us
    psum x1, waiting for transfers between devices, body(): out_grad = lax.psum(out_grad, 'seq').astype(F32)  49.6 us
    all_gather x1, waiting for transfers between devices, body(): lax.all_gather(jnp.concatenate([w_here, small], axis=1), 'wt', axis=0, ti...  48.1 us
    reduce_scatter x1, waiting for transfers between devices, body(): lax.psum_scatter(out_part.astype(BF), 'seq', scatter_dimension=0, tiled=T...  40.4 us
    all_gather x1, waiting for transfers between devices, body(): tokens_all = lax.all_gather(tokens[0], 'seq', axis=0, tiled=True)  39.6 us
  transfers between devices with their start and end apart: 21, of which 19 were waited for; matrix products, arithmetic and copies ran while one was open for 20% of the time, Pallas kernels for 0%

profile of v1, /device:TPU:0, one launch (start us, length us, event | category | flops | bytes accessed | tf_op | source)
XLA Modules:
  0.0 1457.4 jit_solution(14407658807051301885)
XLA Ops:
  18.4 39.6 %all-gather.25.cloned.1.call-done = bf16[1,512,2048]{2,1,0:T(8,128)(2,1)} async-done(((bf16[1,128,2048]{2,1,0:T(8,128)(2,1)}), bf16[1,512,2048]{2,1,0:T(8,128)(2,1)}) %all-gather.25.cloned.1.call-update) | async-done | bytes 2097168 | tf_op jit(solution)/shard_map/all_gather | solution.py:96
  60.1 48.1 %all-gather.19.cloned.1.call-done = bf16[2048,1664]{0,1:T(8,128)(2,1)} async-done(((bf16[256,1664]{0,1:T(8,128)(2,1)}), bf16[2048,1664]{0,1:T(8,128)(2,1)}) %all-gather.19.cloned.1.call-update) | async-done | bytes 6815760 | tf_op jit(solution)/shard_map/all_gather | solution.py:112
  133.7 30.9 %all_to_all.33 = bf16[512,4,128]{2,1,0:T(4,128)(2,1)S(1)} all-to-all(bf16[512,4,128]{2,1,0:T(4,128)(2,1)S(1)} %copy.163), channel_id=1, replica_groups=mesh['seq'=4,'wt'=8] {'seq'}, dimensions={0} | all-to-all | bytes 1048576 | tf_op jit(solution)/shard_map/all_to_all | solution.py:152
  183.6 13.9 all-gather.1
  197.7 19.5 %all-gather.23.cloned.1.call-done = bf16[512,2048]{1,0:T(8,128)(2,1)} async-done(((bf16[128,2048]{1,0:T(8,128)(2,1)}), bf16[512,2048]{1,0:T(8,128)(2,1)}) %all-gather.23.cloned.1.call-update) | async-done | bytes 2097168 | tf_op jit(solution)/shard_map/all_gather | solution.py:160
  222.4 68.0 %all-gather.31.cloned.1.call-done = bf16[3072,2048]{1,0:T(8,128)(2,1)} async-done(((bf16[384,2048]{1,0:T(8,128)(2,1)}), bf16[3072,2048]{1,0:T(8,128)(2,1)}) %all-gather.31.cloned.1.call-update) | async-done | bytes 12582928 | tf_op jit(solution)/shard_map/all_gather | solution.py:116
  304.3 60.5 %all-gather.27.cloned.1.call-done = bf16[3072,2048]{1,0:T(8,128)(2,1)} async-done(((bf16[384,2048]{1,0:T(8,128)(2,1)}), bf16[3072,2048]{1,0:T(8,128)(2,1)}) %all-gather.27.cloned.1.call-update) | async-done | bytes 12582928 | tf_op jit(solution)/shard_map/all_gather | solution.py:116
  378.5 60.2 %all-gather.29.cloned.1.call-done = bf16[3072,2048]{1,0:T(8,128)(2,1)} async-done(((bf16[384,2048]{1,0:T(8,128)(2,1)}), bf16[3072,2048]{1,0:T(8,128)(2,1)}) %all-gather.29.cloned.1.call-update) | async-done | bytes 12582928 | tf_op jit(solution)/shard_map/all_gather | solution.py:116
  452.5 60.1 %all-gather.33.cloned.1.call-done = bf16[3072,2048]{1,0:T(8,128)(2,1)} async-done(((bf16[384,2048]{1,0:T(8,128)(2,1)}), bf16[3072,2048]{1,0:T(8,128)(2,1)}) %all-gather.33.cloned.1.call-update) | async-done | bytes 12582928 | tf_op jit(solution)/shard_map/all_gather | solution.py:116
  526.1 9.6 fusion.110
  583.8 10.7 fusion.39
  594.5 9.7 fusion.41
  611.5 12.3 add_convert_fusion
  642.1 30.1 %reduce-scatter.12.cloned.1.call-done = bf16[128,2080]{1,0:T(8,128)(2,1)} async-done(((bf16[512,2080]{1,0:T(8,128)(2,1)}), bf16[128,2080]{1,0:T(8,128)(2,1)}) %reduce-scatter.12.cloned.1.call-update) | async-done | bytes 532496 | tf_op jit(solution)/shard_map/reduce_scatter | solution.py:215
  677.6 40.4 %reduce-scatter.10.cloned.1.call-done = bf16[128,2048]{1,0:T(8,128)(2,1)} async-done(((bf16[512,2048]{1,0:T(8,128)(2,1)}), bf16[128,2048]{1,0:T(8,128)(2,1)}) %reduce-scatter.10.cloned.1.call-update) | async-done | bytes 524304 | tf_op jit(solution)/shard_map/reduce_scatter | solution.py:225
  737.4 14.1 all-to-all-done.1
  768.3 9.8 fusion.8
  875.6 35.4 %reduce-scatter.14.cloned.1.call-done = bf16[128,2048]{1,0:T(8,128)(2,1)} async-done(((bf16[512,2048]{1,0:T(8,128)(2,1)}), bf16[128,2048]{1,0:T(8,128)(2,1)}) %reduce-scatter.14.cloned.1.call-update) | async-done | bytes 524304 | tf_op jit(solution)/shard_map/reduce_scatter | solution.py:278
  914.8 49.6 %all-reduce.9.cloned.1.call-done = bf16[256,2048]{1,0:T(8,128)(2,1)} async-done(((bf16[256,2048]{1,0:T(8,128)(2,1)}), bf16[256,2048]{1,0:T(8,128)(2,1)}) %all-reduce.9.cloned.1.call-update) | async-done | bytes 1048592 | tf_op jit(solution)/shard_map/psum | solution.py:256
  967.2 92.2 %reduce-scatter.26.cloned.1.call-done = bf16[1,384,2048]{2,1,0:T(8,128)(2,1)} async-done(((bf16[8,384,2048]{2,1,0:T(8,128)(2,1)}), bf16[1,384,2048]{2,1,0:T(8,128)(2,1)}) %reduce-scatter.26.cloned.1.call-update) | async-done | bytes 1572880 | tf_op jit(solution)/shard_map/reduce_scatter | solution.py:203
  1061.1 93.8 %reduce-scatter.24.cloned.1.call-done = bf16[1,384,2048]{2,1,0:T(8,128)(2,1)} async-done(((bf16[8,384,2048]{2,1,0:T(8,128)(2,1)}), bf16[1,384,2048]{2,1,0:T(8,128)(2,1)}) %reduce-scatter.24.cloned.1.call-update) | async-done | bytes 1572880 | tf_op jit(solution)/shard_map/reduce_scatter | solution.py:203
  1159.0 91.7 %reduce-scatter.22.cloned.1.call-done = bf16[1,384,2048]{2,1,0:T(8,128)(2,1)} async-done(((bf16[8,384,2048]{2,1,0:T(8,128)(2,1)}), bf16[1,384,2048]{2,1,0:T(8,128)(2,1)}) %reduce-scatter.22.cloned.1.call-update) | async-done | bytes 1572880 | tf_op jit(solution)/shard_map/reduce_scatter | solution.py:203
  1254.7 91.8 %reduce-scatter.20.cloned.1.call-done = bf16[1,384,2048]{2,1,0:T(8,128)(2,1)} async-done(((bf16[8,384,2048]{2,1,0:T(8,128)(2,1)}), bf16[1,384,2048]{2,1,0:T(8,128)(2,1)}) %reduce-scatter.20.cloned.1.call-update) | async-done | bytes 1572880 | tf_op jit(solution)/shard_map/reduce_scatter | solution.py:203
  1356.2 59.4 %all-gather.37.cloned.1.call-done = bf16[1024,1664]{0,1:T(8,128)(2,1)} async-done(((bf16[256,1664]{0,1:T(8,128)(2,1)}), bf16[1024,1664]{0,1:T(8,128)(2,1)}) %all-gather.37.cloned.1.call-update) | async-done | bytes 3407888 | tf_op jit(solution)/shard_map/all_gather | solution.py:306
  (419 shorter events, 390.0 us)
Async XLA Ops:
  7.2 50.8 %all-gather.25.cloned.1.call-start = ((), (), s32[]{:S(2)}) async-start(), calls=%async_computation.24 | async-start | bytes 2621440 | tf_op jit(solution)/shard_map/all_gather | solution.py:96
  7.9 100.2 %all-gather.19.cloned.1.call-start = ((), (), s32[]{:S(2)}) async-start(), calls=%async_computation.11 | async-start | bytes 7667712 | tf_op jit(solution)/shard_map/all_gather | solution.py:112
  13.8 94.4 %copy-start.73 = (bf16[8,128]{1,0:T(8,128)(2,1)S(1)}, bf16[8,128]{1,0:T(8,128)(2,1)}, u32[]{:S(2)}) copy-start(bf16[8,128]{1,0:T(8,128)(2,1)} %constant.61.clone) | copy-start | bytes 6148
  14.9 150.1 %all-gather.21.cloned.1.call-start = ((), (), s32[]{:S(2)}) async-start(), calls=%async_computation.12 | async-start | bytes 9437184 | tf_op jit(solution)/shard_map/all_gather | solution.py:113
  15.7 201.6 %all-gather.23.cloned.1.call-start = ((), (), s32[]{:S(2)}) async-start(), calls=%async_computation.13 | async-start | bytes 2621440 | tf_op jit(solution)/shard_map/all_gather | solution.py:160
  18.4 106.8 %copy-start.28 = (f32[512,64]{1,0:T(8,128)}, f32[512,64]{1,0:T(8,128)S(1)}, u32[]{:S(2)}) copy-start(f32[512,64]{1,0:T(8,128)S(1)} %get-tuple-element.77) | copy-start | bytes 393220
  172.0 118.5 %all-gather.31.cloned.1.call-start = ((), (), s32[]{:S(2)}) async-start(), calls=%async_computation.27 | async-start | bytes 14155776 | tf_op jit(solution)/shard_map/all_gather | solution.py:116
  176.5 188.2 %all-gather.27.cloned.1.call-start = ((), (), s32[]{:S(2)}) async-start(), calls=%async_computation.25 | async-start | bytes 14155776 | tf_op jit(solution)/shard_map/all_gather | solution.py:116
  178.9 259.7 %all-gather.29.cloned.1.call-start = ((), (), s32[]{:S(2)}) async-start(), calls=%async_computation.26 | async-start | bytes 14155776 | tf_op jit(solution)/shard_map/all_gather | solution.py:116
  181.5 331.1 %all-gather.33.cloned.1.call-start = ((), (), s32[]{:S(2)}) async-start(), calls=%async_computation.28 | async-start | bytes 14155776 | tf_op jit(solution)/shard_map/all_gather | solution.py:116
  182.8 377.0 %all-gather.35.cloned.1.call-start = ((), (), s32[]{:S(2)}) async-start(), calls=%async_computation.29 | async-start | bytes 2621440 | tf_op jit(solution)/shard_map/all_gather | solution.py:114
  183.5 488.6 %reduce-scatter.12.cloned.1.call-start = ((), (), s32[]{:S(2)}) async-start(), calls=%async_computation.15 | async-start | bytes 2785280 | tf_op jit(solution)/shard_map/reduce_scatter | solution.py:215
  197.7 101.1 %copy-start.49 = (pred[512,16]{1,0:T(8,128)(4,1)}, pred[512,16]{1,0:T(8,128)(4,1)S(1)}, u32[]{:S(2)}) copy-start(pred[512,16]{1,0:T(8,128)(4,1)S(1)} %copy.167) | copy-start | bytes 24580
  626.7 91.3 %reduce-scatter.10.cloned.1.call-start = ((), (), s32[]{:S(2)}) async-start(), calls=%async_computation.14 | async-start | bytes 2621440 | tf_op jit(solution)/shard_map/reduce_scatter | solution.py:225
  640.9 156.3 %reduce-scatter.18.cloned.1.call-start = ((), (), s32[]{:S(2)}) async-start(), calls=%async_computation.18 | async-start | bytes 9437184 | tf_op jit(solution)/shard_map/reduce_scatter | solution.py:253
  733.6 17.9 %all-to-all-start.1 = ((bf16[128,16,128]{2,0,1:T(8,128)(2,1)}), bf16[128,16,128]{2,0,1:T(8,128)(2,1)S(1)}, u32[]{:S(2)}, u32[]{:S(2)}) async-start(bf16[128,16,128]{2,0,1:T(8,128)(2,1)} %bitcast.275), calls=%async_computation.3 | async-start | bytes 1048576 | tf_op jit(solution)/shard_map/all_to_all | solution.py:251
  737.1 137.4 %reduce-scatter.16.cloned.1.call-start = ((), (), s32[]{:S(2)}) async-start(), calls=%async_computation.17 | async-start | bytes 7667712 | tf_op jit(solution)/shard_map/reduce_scatter | solution.py:300
  791.9 119.1 %reduce-scatter.14.cloned.1.call-start = ((), (), s32[]{:S(2)}) async-start(), calls=%async_computation.16 | async-start | bytes 2621440 | tf_op jit(solution)/shard_map/reduce_scatter | solution.py:278
  792.5 171.9 %all-reduce.9.cloned.1.call-start = ((), (), s32[]{:S(2)}) async-start(), calls=%async_computation.19 | async-start | bytes 2097152 | tf_op jit(solution)/shard_map/psum | solution.py:256
  797.2 262.2 %reduce-scatter.26.cloned.1.call-start = ((), (), s32[]{:S(2)}) async-start(), calls=%async_computation.23 | async-start | bytes 14155776 | tf_op jit(solution)/shard_map/reduce_scatter | solution.py:203
  815.9 339.1 %reduce-scatter.24.cloned.1.call-start = ((), (), s32[]{:S(2)}) async-start(), calls=%async_computation.22 | async-start | bytes 14155776 | tf_op jit(solution)/shard_map/reduce_scatter | solution.py:203
  835.4 415.3 %reduce-scatter.22.cloned.1.call-start = ((), (), s32[]{:S(2)}) async-start(), calls=%async_computation.21 | async-start | bytes 14155776 | tf_op jit(solution)/shard_map/reduce_scatter | solution.py:203
  855.0 491.5 %reduce-scatter.20.cloned.1.call-start = ((), (), s32[]{:S(2)}) async-start(), calls=%async_computation.20 | async-start | bytes 14155776 | tf_op jit(solution)/shard_map/reduce_scatter | solution.py:203
  874.4 541.2 %all-gather.37.cloned.1.call-start = ((), (), s32[]{:S(2)}) async-start(), calls=%async_computation.30 | async-start | bytes 4259840 | tf_op jit(solution)/shard_map/all_gather | solution.py:306
  (103 other events, 1002.9 us)
Sparse Core Ops, SparseCore 0:
  9.6 48.3 all-gather.24
  60.4 47.6 all-gather.18
  110.1 54.2 all-gather.20
  172.1 45.1 all-gather.22
  219.6 70.7 all-gather.30
  292.7 71.9 all-gather.26
  366.7 71.9 all-gather.28
  440.6 71.9 all-gather.32
  514.2 45.6 all-gather.34
  626.8 45.2 reduce-scatter.11
  675.0 42.9 reduce-scatter.9
  726.4 70.6 reduce-scatter.17
  800.6 64.0 reduce-scatter.15
  867.4 43.5 reduce-scatter.13
  913.2 51.0 all-reduce.8
  967.7 91.5 reduce-scatter.25
  1062.7 92.2 reduce-scatter.23
  1158.3 92.2 reduce-scatter.21
  1254.2 92.2 reduce-scatter.19
  1347.9 67.6 all-gather.36
